TPU v7x, 32 devices: a whole 2x2x4 slice. The times are simulated.
32 devices in a mesh: stream: 32 (over z, y, x, core), item: 1.
Axes of the slice: x: 2, y: 2, z: 4, core: 2. Of those that a mesh axis runs over, the one named last changes fastest.
Arguments:
- event_items: int32 [131072], P('stream'), may hold values from 0 to 262143, as said below
- event_sessions: int32 [131072], P('stream'), may hold values from 0 to 8191, never falling along the last dimension, each value on 1 to 64 neighbouring positions
- sketch_bits: int32 [15, 262144], P(None, 'item'), may hold values from 0 to 262143
Outputs:
- sketch: float32 [128, 256], P('stream')
Inputs may be any that keep to these rules, and one draw needn't show every extreme that they name: `event_items`: item 262144 - 1 occurs at least once.
All inputs are finite; a program needn't handle non-finite values.
Results may differ from a plain program's by a relative error of at most 0.0006.
Values may be sent and summed in bfloat16 or wider, within the bound.
A program may use at most 128 MiB of HBM per device.

v0:
```python
import functools
import math

import jax
import jax.numpy as jnp
from jax import lax
from jax.experimental import pallas as pl
from jax.experimental.pallas import tpu as pltpu
from jax.sharding import PartitionSpec as P

WINDOW = 15
ITEM_BITS = 18
LANES = 128
BITS_PER_WORD = 18
BIG = 1.0e6
VMEM_GRANT = 45 * 1024 * 1024
NT = (((1,), (1,)), ((), ()))
VMEM = pl.BlockSpec(memory_space=pltpu.VMEM)


def one_where(mask):
    return jnp.where(mask, 1.0, 0.0).astype(jnp.bfloat16)


def hot_columns(ids, values):
    row = jnp.broadcast_to(values, (16, values.shape[1])).astype(jnp.bfloat16)
    one, zero = jnp.ones((), jnp.bfloat16), jnp.zeros((), jnp.bfloat16)
    return jnp.concatenate(
        [jnp.where(ids[n : n + 16] == row, one, zero) for n in range(0, ids.shape[0], 16)], axis=0
    )


def greet_all(slabs, me):
    barrier = pltpu.get_barrier_semaphore()

    for k in range(1, slabs):
        pl.semaphore_signal(
            barrier, inc=1, device_id={"stream": lax.rem(me + k, slabs)}, device_id_type=pl.DeviceIdType.MESH
        )
    return barrier


def send(src, dst, send_sem, recv_sem, to):
    return pltpu.make_async_remote_copy(
        src_ref=src,
        dst_ref=dst,
        send_sem=send_sem,
        recv_sem=recv_sem,
        device_id={"stream": to},
        device_id_type=pl.DeviceIdType.MESH,
    )


def each(low, high, do):
    for k in range(low, high):
        do(k)


def exchange(slabs, me, out_ref, in_ref, send_sems, recv_sems, start):
    def copy(k):
        to = lax.rem(me + k, slabs)
        return send(out_ref.at[to], in_ref.at[me], send_sems.at[k], recv_sems.at[k], to)

    if start:
        each(1, slabs, lambda k: copy(k).start())
        in_ref[me] = out_ref[me]
    else:
        each(1, slabs, lambda k: copy(k).wait())


def gather_kernel(
    slabs, rows, blocks, own_ref, all_items, all_sessions, head_ref,
    short_ref, halo_ref, item_ref, session_ref, links_ref, total_ref,
    head_out, head_in, far_send, far_recv, near_send, near_recv, halo_send, halo_recv, head_send, head_recv,
):
    me = lax.axis_index("stream")
    partner = me + 1 - 2 * lax.rem(me, 2)
    after, before = lax.rem(me + 1, slabs), lax.rem(me + slabs - 1, slabs)
    own_items, own_sessions = own_ref.at[0], own_ref.at[1]
    barrier = greet_all(slabs, me)
    short_ref[...] = own_sessions[...].astype(jnp.int16)
    item_ref[8 : 8 + blocks] = own_items[...]
    session_ref[8 : 8 + blocks] = own_sessions[...]
    all_items[me] = own_items[...]
    all_sessions[me] = short_ref[...]
    pl.semaphore_wait(barrier, slabs - 1)

    halos = []
    for n, ref in enumerate((own_items, own_sessions)):
        for side, to, rows_sent in ((0, after, ref.at[blocks - 8 : blocks]), (1, before, ref.at[0:8])):
            at = 2 * n + side
            halos.append(send(rows_sent, halo_ref.at[at], halo_send.at[at], halo_recv.at[at], to))
    for copy in halos:
        copy.start()

    pairs = ((own_items, all_items, 0), (short_ref, all_sessions, slabs // 2))

    def far(k):
        to = lax.rem(me + 2 * k, slabs)
        return [
            send(own, every.at[me], far_send.at[at + k], far_recv.at[at + k], to) for own, every, at in pairs
        ]

    def near(k):
        source = lax.rem(me + 2 * slabs - 2 * k, slabs)
        return [
            send(every.at[source], every.at[source], near_send.at[at + k], near_recv.at[at + k], partner)
            for own, every, at in pairs
        ]

    def do_all(copies, act):
        for copy in copies:
            act(copy)

    own_near = [
        send(own, every.at[me], near_send.at[at], near_recv.at[at], partner) for own, every, at in pairs
    ]
    each(1, slabs // 2, lambda k: do_all(far(k), lambda c: c.start()))
    do_all(own_near, lambda c: c.start())

    sub = lax.broadcasted_iota(jnp.int32, (LANES, LANES), 0)
    lane = lax.broadcasted_iota(jnp.int32, (LANES, LANES), 1)
    low_lane = lax.broadcasted_iota(jnp.int32, (1, LANES), 1) < LANES // 2
    ids = lax.broadcasted_iota(jnp.int32, (rows, LANES), 0)
    gaps = (sub - LANES // 2 - lane, sub + LANES // 2 - lane)
    in_reach = [(jnp.abs(gap) <= WINDOW) & (gap != 0) for gap in gaps]
    ones = jnp.ones((8, 2 * LANES), jnp.float32).astype(jnp.bfloat16)
    links_ref[...] = jnp.zeros_like(links_ref)
    total_ref[...] = jnp.zeros_like(total_ref)

    def block(b, unused):
        def around(ref):
            turned = [pltpu.roll(ref[pl.ds(b + o, 1)], LANES // 2, 1) for o in (7, 8, 9)]
            return (
                jnp.where(low_lane, turned[0], turned[1]),
                jnp.where(low_lane, turned[1], turned[2]),
            )

        own_item, own_session = item_ref[pl.ds(b + 8, 1)], session_ref[pl.ds(b + 8, 1)]
        hot = jnp.concatenate([one_where(ids == item) for item in around(item_ref)], axis=1)
        linked = jnp.concatenate(
            [
                one_where((jnp.broadcast_to(session, (LANES, LANES)).T == own_session) & reach)
                for session, reach in zip(around(session_ref), in_reach)
            ],
            axis=0,
        )
        links = jnp.dot(jnp.concatenate([hot, ones], axis=0), linked, preferred_element_type=jnp.float32)
        links_ref[...] += lax.dot_general(
            links.astype(jnp.bfloat16), one_where(ids == own_item), NT, preferred_element_type=jnp.float32
        )
        total_ref[...] += links[rows:]
        return unused

    lax.fori_loop(1, blocks - 1, block, 0, unroll=5)
    for copy in halos:
        copy.wait()
    item_ref[0:8] = halo_ref[0]
    item_ref[8 + blocks : 16 + blocks] = halo_ref[1]
    session_ref[0:8] = jnp.where(me == 0, -1, halo_ref[2])
    session_ref[8 + blocks : 16 + blocks] = jnp.where(me == slabs - 1, -1, halo_ref[3])
    block(0, 0)
    block(blocks - 1, 0)

    share = rows // slabs
    tail = jnp.concatenate([links_ref[rows : rows + 1], total_ref[0:1]], axis=0)
    for d in range(slabs):
        head_out[d, 0:share] = links_ref[d * share : (d + 1) * share]
        head_out[d, share : share + 2] = tail
        head_out[d, share + 2 : 8] = jnp.zeros((6 - share, LANES), jnp.float32)

    exchange(slabs, me, head_out, head_in, head_send, head_recv, True)

    def forward(k):
        do_all(far(k), lambda c: c.wait_recv())
        do_all(near(k), lambda c: c.start())

    each(1, slabs // 2, forward)
    exchange(slabs, me, head_out, head_in, head_send, head_recv, False)
    head_ref[...] = jnp.sum(head_in[...], axis=0)
    do_all(own_near, lambda c: c.wait())
    each(1, slabs // 2, lambda k: do_all(near(k), lambda c: c.wait()))
    each(1, slabs // 2, lambda k: do_all(far(k), lambda c: c.wait_send()))


def take_windows(code_ref, length, start):
    whole, part = start >> 3, start & 7
    bits = max(1, (length // 8 - 1).bit_length())
    keep = 8 * ((1 << (bits - 1)) + 4)
    value = None
    for bit in reversed(range(bits)):
        step = 8 << bit
        keep = 8 * ((1 << bit) + 4)
        chosen = ((whole >> bit) & 1) == 1
        if value is None:
            low, high = code_ref[0:keep, :], code_ref[step : step + keep, :]
        else:
            low, high = value[0:keep], value[step : step + keep]
        value = jnp.where(chosen, high, low)
    for bit in (2, 1, 0):
        chosen = ((part >> bit) & 1) == 1
        value = jnp.where(chosen, pltpu.roll(value, value.shape[0] - (1 << bit), 0), value)
    return value[0:32]


def tile_kernel(rows, length, half, base_ref, all_items, all_sessions, count_ref, margin_ref, flat_ref, code_ref, key_ref):
    item_mask = (1 << ITEM_BITS) - 1
    base = base_ref[0]
    count_ref[...] = jnp.zeros_like(count_ref)
    margin_ref[...] = jnp.zeros_like(margin_ref)
    band = 2 * half
    band_rows = band // LANES
    chunk = 8 * math.gcd(length // 8, 16)
    slabs, blocks, unused_lanes = all_items.shape
    for n in range(slabs):
        flat_ref[n * blocks : (n + 1) * blocks] = all_items[n] | (all_sessions[n].astype(jnp.int32) << ITEM_BITS)
    per = length // LANES
    for r in range(per):
        code_ref[16 + r * LANES : 16 + (r + 1) * LANES] = flat_ref[pl.ds(r, LANES, stride=per), :].T
    lane = lax.broadcasted_iota(jnp.int32, (16, LANES), 1)
    code_ref[0:16] = jnp.where(lane == 0, -1, pltpu.roll(code_ref[length : length + 16], 1, 1))
    code_ref[length + 16 : length + 32] = jnp.where(
        lane == LANES - 1, -1, pltpu.roll(code_ref[16:32], LANES - 1, 1)
    )

    def fill(c, tops):
        at = pl.multiple_of(c * chunk, chunk)
        item = code_ref[pl.ds(at + 16, chunk), :] & item_mask
        place = (at + lax.broadcasted_iota(jnp.int32, (chunk, LANES), 0)).astype(jnp.float32)
        new = []
        for s in range(2):
            local = item - base - s * band
            mine = (local >= 0) & (local < band) & (item >= rows)
            key_ref[s, pl.ds(at, chunk), :] = jnp.where(mine, place, BIG)
            new.append(tops[s] + jnp.sum(mine.astype(jnp.int32), axis=0, keepdims=True))
        return tuple(new)

    none = jnp.zeros((1, LANES), jnp.int32)
    tally = lax.fori_loop(0, length // chunk, fill, (none, none))
    trips = (jnp.max(jnp.maximum(tally[0], tally[1])) + 1) // 2

    row_ids = lax.broadcasted_iota(jnp.int32, (rows, 2 * LANES), 0).astype(jnp.float32).astype(jnp.bfloat16)
    d_ids = lax.broadcasted_iota(jnp.int32, (32, LANES), 0)
    near = (d_ids >= 1) & (d_ids != 16)
    m_ids = lax.broadcasted_iota(jnp.int32, (max(8, band_rows), 2 * LANES), 0)
    l_ids = lax.broadcasted_iota(jnp.int32, (LANES, 2 * LANES), 0)
    tile = 256
    t_ids = lax.broadcasted_iota(jnp.int32, (tile, 2 * LANES), 0).astype(jnp.float32).astype(jnp.bfloat16)

    def body(unused, state):
        out = []
        for s in range(2):
            first, last = state[2 * s], state[2 * s + 1]
            key = key_ref[s]
            next_first = jnp.min(jnp.where(key > first, key, BIG), axis=0, keepdims=True)
            next_last = jnp.max(jnp.where(key < last, key, -1.0), axis=0, keepdims=True)
            first_ok = next_first < last
            last_ok = next_last > next_first
            out += [next_first, next_last]
            heads, weights, locals_ = [], [], []
            for at, ok in ((next_first, first_ok), (next_last, last_ok)):
                start = jnp.where(ok, at, 0.0).astype(jnp.int32)
                window = take_windows(code_ref, length, start)
                item, session = window & item_mask, window >> ITEM_BITS
                linked = (session == session[16:17]) & near & ok
                heads.append(jnp.where(linked & (item < rows), item, -1).astype(jnp.float32))
                weights.append(jnp.sum(jnp.where(linked, 1.0, 0.0), axis=0, keepdims=True))
                locals_.append(item[16:17] - base - s * band)
            head = jnp.concatenate(heads, axis=1)
            weight = jnp.concatenate(weights, axis=1)
            local = jnp.concatenate(locals_, axis=1)
            links = jnp.zeros((rows, 2 * LANES), jnp.bfloat16)
            for d in range(1, 32):
                if d != 16:
                    links += hot_columns(row_ids, head[d : d + 1])
            upper = local >= half
            side = jnp.broadcast_to(jnp.where(upper, 1.0, 0.0), (16, 2 * LANES)).astype(jnp.bfloat16)
            high_part = jnp.concatenate([links[n : n + 16] * side for n in range(0, rows, 16)], axis=0)
            pair = jnp.concatenate([links - high_part, high_part], axis=0)
            inner = jnp.where(upper, local - half, local)
            for t in range(half // tile):
                inside = (inner >= t * tile) & (inner < (t + 1) * tile)
                hot = hot_columns(t_ids, jnp.where(inside, inner - t * tile, -1).astype(jnp.float32))
                count_ref[s, :, t * tile : (t + 1) * tile] += lax.dot_general(
                    pair, hot, NT, preferred_element_type=jnp.float32
                )
            coarse = jnp.where(m_ids == (local >> 7), weight, 0.0).astype(jnp.bfloat16)
            fine = one_where(l_ids == (local & (LANES - 1)))
            margin_ref[s] += lax.dot_general(coarse, fine, NT, preferred_element_type=jnp.float32)
        return tuple(out)

    low = jnp.full((1, LANES), -1.0, jnp.float32)
    high = jnp.full((1, LANES), BIG, jnp.float32)
    lax.fori_loop(0, trips, body, (low, high, low, high))


def sketch_kernel(
    slabs, rows, half, width, scale, count_ref, margin_ref, head_ref, bits_ref, out_ref,
    log_ref, own_bits, head_bits, acc_ref, send_ref, recv_ref, bit_sems, send_sems, recv_sems,
):
    me = lax.axis_index("stream")
    barrier = greet_all(slabs, me)
    owned = 4 * half
    share = rows // slabs
    tile = min(half, 512)
    bit_copy = pltpu.make_async_copy(
        bits_ref.at[:, pl.ds(pl.multiple_of(me * owned, owned), owned)], own_bits, bit_sems.at[0]
    )
    head_copy = pltpu.make_async_copy(bits_ref.at[:, 0:rows], head_bits, bit_sems.at[1])
    bit_copy.start()
    head_copy.start()

    log_ref[...] = jnp.log(jnp.maximum(margin_ref[...], 1.0))
    row_log = jnp.log(jnp.maximum(head_ref[share : share + 1], 1.0))
    column_log = jnp.broadcast_to(row_log, (rows, LANES)).T
    total_log = jnp.log(jnp.sum(head_ref[share + 1 : share + 2], axis=1, keepdims=True))
    row_term = total_log - column_log[:, 0:1]
    groups = []
    for g in range(width // 8):
        word = 8 * g // BITS_PER_WORD
        groups.append((word, (word + 1) * BITS_PER_WORD - 8 * g, 8 * g - word * BITS_PER_WORD))

    def product(positive, words):
        size = words.shape[1]

        def wide(value):
            return jnp.concatenate([value] * (size // LANES), axis=1)

        shift = lax.broadcasted_iota(jnp.int32, (8, LANES), 0)
        upper = positive.astype(jnp.bfloat16)
        lower = (positive - upper.astype(jnp.float32)).astype(jnp.bfloat16)
        parts = []
        for word, split, offset in groups:
            now = jnp.broadcast_to(words[word : word + 1], (8, size))
            where_bit = jnp.left_shift(1, shift + offset)
            if split < 8:
                later = jnp.broadcast_to(words[word + 1 : word + 2], (8, size))
                now = jnp.where(wide(shift) >= split, later, now)
                place = jnp.where(shift >= split, shift - split, shift + offset)
                where_bit = jnp.left_shift(1, place)
            parts.append(jnp.where((now & wide(where_bit)) != 0, 1.0, -1.0))
        signs = jnp.concatenate(parts, axis=0).astype(jnp.bfloat16)
        both = jnp.concatenate([upper, lower], axis=0)
        value = lax.dot_general(both, signs, NT, preferred_element_type=jnp.float32)
        return value[0:rows] + value[rows:]

    head_copy.wait()
    row = lax.broadcasted_iota(jnp.int32, (8, LANES), 0)
    shared = jnp.concatenate(
        [jnp.where(row < share, head_ref[...], 0.0), jnp.zeros((rows - 8, LANES), jnp.float32)], axis=0
    )
    shared = pltpu.roll(shared, me * share, 0)
    ratio = jnp.log(jnp.maximum(shared, 1.0)) + total_log - row_log - column_log
    first_band = jnp.where(lax.axis_index("item") == 0, 1.0, 0.0)
    positive = jnp.where(shared > 0, jnp.maximum(ratio, 0.0), 0.0) * first_band
    acc_ref[...] = product(positive.T, head_bits[...])
    bit_copy.wait()

    for s in range(2):
        for h in range(2):

            def step(t, unused, s=s, h=h):
                at = pl.multiple_of(t * tile, tile)
                counts = count_ref[s, h * rows : (h + 1) * rows, pl.ds(at, tile)]
                first_log = h * (half // LANES) + t * (tile // LANES)
                col_log = jnp.concatenate(
                    [log_ref[s, pl.ds(first_log + n, 1), :] for n in range(tile // LANES)], axis=1
                )
                ratio = jnp.log(jnp.maximum(counts, 1.0)) + row_term - col_log
                positive = jnp.where(counts > 0, jnp.maximum(ratio, 0.0), 0.0)
                bit_at = pl.multiple_of(s * 2 * half + h * half + t * tile, tile)
                acc_ref[...] += product(positive, own_bits[:, pl.ds(bit_at, tile)])
                return unused

            lax.fori_loop(0, half // tile, step, 0, unroll=True)

    cuts = width // LANES
    for d in range(slabs):
        for c in range(cuts):
            send_ref[d, c * share : (c + 1) * share] = (
                acc_ref[d * share : (d + 1) * share, c * LANES : (c + 1) * LANES] * scale
            )
    pl.semaphore_wait(barrier, slabs - 1)
    exchange(slabs, me, send_ref, recv_ref, send_sems, recv_sems, True)
    exchange(slabs, me, send_ref, recv_ref, send_sems, recv_sems, False)
    summed = jnp.sum(recv_ref[...], axis=0)
    out_ref[...] = jnp.concatenate([summed[c * share : (c + 1) * share] for c in range(cuts)], axis=1)


def local(event_items, event_sessions, sketch_bits):
    slabs = lax.axis_size("stream")
    slab = event_items.shape[0]
    total_events = slab * slabs
    words, band_size = sketch_bits.shape
    owned = band_size // slabs
    rows, width, half = 128, 256, owned // 4
    me = lax.axis_index("stream")
    own_start = me * owned
    first_id = lax.axis_index("item") * band_size + own_start
    blocks = slab // LANES
    length = total_events // LANES

    dma = pltpu.SemaphoreType.DMA
    all_items, all_sessions, head = pl.pallas_call(
        functools.partial(gather_kernel, slabs, rows, blocks),
        out_shape=(
            jax.ShapeDtypeStruct((slabs, blocks, LANES), jnp.int32),
            jax.ShapeDtypeStruct((slabs, blocks, LANES), jnp.int16),
            jax.ShapeDtypeStruct((8, LANES), jnp.float32),
        ),
        in_specs=[VMEM],
        out_specs=(VMEM, VMEM, VMEM),
        scratch_shapes=[
            pltpu.VMEM((blocks, LANES), jnp.int16),
            pltpu.VMEM((4, 8, LANES), jnp.int32),
            pltpu.VMEM((blocks + 16, LANES), jnp.int32),
            pltpu.VMEM((blocks + 16, LANES), jnp.int32),
            pltpu.VMEM((rows + 8, LANES), jnp.float32),
            pltpu.VMEM((8, LANES), jnp.float32),
            pltpu.VMEM((slabs, 8, LANES), jnp.float32),
            pltpu.VMEM((slabs, 8, LANES), jnp.float32),
            dma((slabs,)),
            dma((slabs,)),
            dma((slabs,)),
            dma((slabs,)),
            dma((4,)),
            dma((4,)),
            dma((slabs,)),
            dma((slabs,)),
        ],
        compiler_params=pltpu.CompilerParams(
            collective_id=0, has_side_effects=True, vmem_limit_bytes=VMEM_GRANT
        ),
        name="gather_events",
    )(jnp.stack([event_items, event_sessions]).reshape(2, blocks, LANES))

    band_rows = max(8, 2 * half // LANES)
    counts, margins = pl.pallas_call(
        functools.partial(tile_kernel, rows, length, half),
        out_shape=(
            jax.ShapeDtypeStruct((2, 2 * rows, half), jnp.float32),
            jax.ShapeDtypeStruct((2, band_rows, LANES), jnp.float32),
        ),
        in_specs=[pl.BlockSpec(memory_space=pltpu.SMEM), VMEM, VMEM],
        out_specs=(VMEM, VMEM),
        scratch_shapes=[
            pltpu.VMEM((length, LANES), jnp.int32),
            pltpu.VMEM((length + 32, LANES), jnp.int32),
            pltpu.VMEM((2, length, LANES), jnp.float32),
        ],
        compiler_params=pltpu.CompilerParams(vmem_limit_bytes=VMEM_GRANT),
        name="tile_counts",
    )(first_id.astype(jnp.int32)[None], all_items, all_sessions)

    own_rows = pl.pallas_call(
        functools.partial(sketch_kernel, slabs, rows, half, width, 1.0 / math.sqrt(total_events)),
        out_shape=jax.ShapeDtypeStruct((rows // slabs, width), jnp.float32),
        in_specs=[VMEM] * 3 + [pl.BlockSpec(memory_space=pl.ANY)],
        out_specs=VMEM,
        scratch_shapes=[
            pltpu.VMEM((2, band_rows, LANES), jnp.float32),
            pltpu.VMEM((words, owned), jnp.int32),
            pltpu.VMEM((words, rows), jnp.int32),
            pltpu.VMEM((rows, width), jnp.float32),
            pltpu.VMEM((slabs, 8, LANES), jnp.float32),
            pltpu.VMEM((slabs, 8, LANES), jnp.float32),
            dma((2,)),
            dma((slabs,)),
            dma((slabs,)),
        ],
        compiler_params=pltpu.CompilerParams(
            collective_id=1, has_side_effects=True, vmem_limit_bytes=VMEM_GRANT
        ),
        name="sketch_tile",
    )(counts, margins, head, sketch_bits)
    if lax.axis_size("item") > 1:
        own_rows = lax.psum(own_rows, "item")
    return own_rows


def solution(mesh):
    placed = (P("stream"), P("stream"), P(None, "item"))
    return jax.shard_map(
        local, mesh=mesh, in_specs=placed, out_specs=P("stream", None), check_vma=False
    )
```

profile of v0, /device:TPU:0, one launch (start us, length us, event | category | flops | bytes accessed | tf_op | source)
XLA Modules:
  0.0 50.5 jit_solution(5317546242454766697)
XLA Ops:
  0.0 0.7 %pad_add_fusion.own_ref = s32[2,32,128]{2,1,0:T(8,128)S(1)} fusion(s32[1,32,128]{2,1,0:T(8,128)} %bitcast.3, s32[1,32,128]{2,1,0:T(8,128)} %bitcast.4), kind=kLoop, calls=%fused_computation | loop fusion | flops 8192 | bytes 65536 | tf_op jit(solution)/shard_map/stack | solution.py:435
  0.7 20.9 %gather_events.1 = (s32[32,32,128]{2,1,0:T(8,128)S(1)}, s16[32,32,128]{2,1,0:T(8,128)(2,1)S(1)}, f32[8,128]{1,0:T(8,128)S(1)}) custom-call(s32[2,32,128]{2,1,0:T(8,128)S(1)} %pad_add_fusion.own_ref), custom_call_target="tpu_custom_call" | custom-call | tf_op jit(solution)/shard_map/gather_events/pallas_call | solution.py:404
  21.7 15.8 %tile_counts.1 = (f32[2,256,2048]{2,1,0:T(8,128)S(1)}, f32[2,32,128]{2,1,0:T(8,128)S(1)}) custom-call(s32[1]{0:T(128)} %bitcast.base_ref, s32[32,32,128]{2,1,0:T(8,128)S(1)} %get-tuple-element.10.all_items, s16[32,32,128]{2,1,0:T(8,128)(2,1)S(1)} %get-tuple-element.11.all_sessions), custom_call_target="tpu_custom_call" | custom-call | tf_op jit(solution)/shard_map/tile_counts/pallas_call | solution.py:438
  37.5 12.4 %sketch_tile.1 = f32[4,256]{1,0:T(4,128)S(1)} custom-call(f32[2,256,2048]{2,1,0:T(8,128)S(1)} %get-tuple-element.12.count_ref, f32[2,32,128]{2,1,0:T(8,128)S(1)} %get-tuple-element.13.margin_ref, f32[8,128]{1,0:T(8,128)S(1)} %get-tuple-element.14.head_ref, s32[15,262144]{1,0:T(8,128)} %bits_ref.1), custom_call_target="tpu_custom_call" | custom-call | tf_op jit(solution)/shard_map/sketch_tile/pallas_call | solution.py:455
  49.9 0.6 %copy.5 = f32[4,256]{1,0:T(4,128)} copy(f32[4,256]{1,0:T(4,128)S(1)} %sketch_tile.1) | data formatting | bytes 8192
where the time goes:
time: 50.5 us
  Pallas kernels  49.1 us (97%)
  other arithmetic  0.74 us (1%)
  local copies, waits for them, and re-layouts  0.6 us (1%)
    pallas_call x1, Pallas kernels, local(): pl.pallas_call(functools.partial(gather_kernel, slabs, rows, blocks), out...  20.9 us
    pallas_call x1, Pallas kernels, local(): pl.pallas_call(functools.partial(tile_kernel, rows, length, half), out_sh...  15.8 us
    pallas_call x1, Pallas kernels, local(): pl.pallas_call(functools.partial(sketch_kernel, slabs, rows, half, width,...  12.4 us

commit v1 on v0

--- a/solution.py
+++ b/solution.py
@@ -13,6 +13,7 @@
 LANES = 128
 BITS_PER_WORD = 18
 BIG = 1.0e6
+PLANE = 8
 VMEM_GRANT = 45 * 1024 * 1024
 NT = (((1,), (1,)), ((), ()))
 VMEM = pl.BlockSpec(memory_space=pltpu.VMEM)
@@ -69,55 +70,45 @@
 
 
 def gather_kernel(
-    slabs, rows, blocks, own_ref, all_items, all_sessions, head_ref,
-    short_ref, halo_ref, item_ref, session_ref, links_ref, total_ref,
-    head_out, head_in, far_send, far_recv, near_send, near_recv, halo_send, halo_recv, head_send, head_recv,
+    slabs, rows, blocks, own_ref, all_ref, head_ref,
+    own_pack, halo_ref, item_ref, session_ref, links_ref, total_ref,
+    pair_out, pair_in, plane_out, plane_in, line_out, line_in,
+    halo_send, halo_recv, line_send, line_recv, plane_send, plane_recv, near_send, near_recv,
+    pair_sems, head_plane_send, head_plane_recv, head_line_send, head_line_recv,
 ):
     me = lax.axis_index("stream")
-    partner = me + 1 - 2 * lax.rem(me, 2)
+    depth = slabs // PLANE
+    layer, low = me // PLANE, lax.rem(me, PLANE)
+    parity, quad = lax.rem(me, 2), lax.rem(me // 2, 4)
+
+    def flip(bit):
+        return bit - 2 * bit * lax.rem(me // bit, 2)
+
+    partner = me + flip(1)
+    steps = (flip(2), flip(4), flip(2) + flip(4))
     after, before = lax.rem(me + 1, slabs), lax.rem(me + slabs - 1, slabs)
+
+    def other_layer(k):
+        rising = k + (k - layer + depth) // depth
+        mirrored = depth - 1 - layer
+        falling = depth - 1 - k - (k - mirrored + depth) // depth
+        high = layer // ((depth + 1) // 2)
+        return rising + (falling - rising) * lax.rem(high, 2)
+
+    others = [other_layer(k) for k in range(depth - 1)]
     own_items, own_sessions = own_ref.at[0], own_ref.at[1]
-    barrier = greet_all(slabs, me)
-    short_ref[...] = own_sessions[...].astype(jnp.int16)
+    barrier = pltpu.get_barrier_semaphore()
+    greeted = [partner, after, before] + [me + step for step in steps] + [o * PLANE + low for o in others]
+    for to in greeted:
+        pl.semaphore_signal(
+            barrier, inc=1, device_id={"stream": to}, device_id_type=pl.DeviceIdType.MESH
+        )
+    half = blocks // 2
+    own_pack[0:blocks] = own_items[...]
+    own_pack[blocks : blocks + half] = own_sessions[0:half] | (own_sessions[half:blocks] << 16)
+    all_ref[me] = own_pack[...]
     item_ref[8 : 8 + blocks] = own_items[...]
     session_ref[8 : 8 + blocks] = own_sessions[...]
-    all_items[me] = own_items[...]
-    all_sessions[me] = short_ref[...]
-    pl.semaphore_wait(barrier, slabs - 1)
-
-    halos = []
-    for n, ref in enumerate((own_items, own_sessions)):
-        for side, to, rows_sent in ((0, after, ref.at[blocks - 8 : blocks]), (1, before, ref.at[0:8])):
-            at = 2 * n + side
-            halos.append(send(rows_sent, halo_ref.at[at], halo_send.at[at], halo_recv.at[at], to))
-    for copy in halos:
-        copy.start()
-
-    pairs = ((own_items, all_items, 0), (short_ref, all_sessions, slabs // 2))
-
-    def far(k):
-        to = lax.rem(me + 2 * k, slabs)
-        return [
-            send(own, every.at[me], far_send.at[at + k], far_recv.at[at + k], to) for own, every, at in pairs
-        ]
-
-    def near(k):
-        source = lax.rem(me + 2 * slabs - 2 * k, slabs)
-        return [
-            send(every.at[source], every.at[source], near_send.at[at + k], near_recv.at[at + k], partner)
-            for own, every, at in pairs
-        ]
-
-    def do_all(copies, act):
-        for copy in copies:
-            act(copy)
-
-    own_near = [
-        send(own, every.at[me], near_send.at[at], near_recv.at[at], partner) for own, every, at in pairs
-    ]
-    each(1, slabs // 2, lambda k: do_all(far(k), lambda c: c.start()))
-    do_all(own_near, lambda c: c.start())
-
     sub = lax.broadcasted_iota(jnp.int32, (LANES, LANES), 0)
     lane = lax.broadcasted_iota(jnp.int32, (LANES, LANES), 1)
     low_lane = lax.broadcasted_iota(jnp.int32, (1, LANES), 1) < LANES // 2
@@ -152,7 +143,59 @@
         total_ref[...] += links[rows:]
         return unused
 
-    lax.fori_loop(1, blocks - 1, block, 0, unroll=5)
+    inner = [1 + (blocks - 2) * n // 30 for n in (0, 15, 30)]
+
+    def blocks_of(n):
+        lax.fori_loop(inner[n], inner[n + 1], block, 0, unroll=5)
+
+    blocks_of(0)
+    pl.semaphore_wait(barrier, len(greeted))
+
+    halos = []
+    for n, ref in enumerate((own_items, own_sessions)):
+        for side, to, rows_sent in ((0, after, ref.at[blocks - 8 : blocks]), (1, before, ref.at[0:8])):
+            at = 2 * n + side
+            halos.append(send(rows_sent, halo_ref.at[at], halo_send.at[at], halo_recv.at[at], to))
+
+    def do_all(copies, act):
+        for copy in copies:
+            act(copy)
+
+    def along_line(there, here):
+        return send(
+            own_pack, all_ref.at[me], line_send.at[there], line_recv.at[here], there * PLANE + low
+        )
+
+    def in_plane(d, at_layer, own=False):
+        slab = all_ref.at[at_layer * PLANE + low]
+        sem = d * depth + at_layer
+        return send(own_pack if own else slab, slab, plane_send.at[sem], plane_recv.at[sem], me + steps[d])
+
+    def to_partner(r, at_layer, own=False):
+        slab = all_ref.at[at_layer * PLANE + low + ((0,) + steps)[r]]
+        sem = r * depth + at_layer
+        return send(own_pack if own else slab, slab, near_send.at[sem], near_recv.at[sem], partner)
+
+    do_all(halos, lambda c: c.start())
+    for o in reversed(others):
+        along_line(o, layer).start()
+    for d in range(3):
+        in_plane(d, layer, True).start()
+    to_partner(0, layer, True).start()
+
+    def forward_line(k):
+        along_line(layer, others[k]).wait_recv()
+        for d in range(3):
+            in_plane(d, others[k]).start()
+        to_partner(0, others[k]).start()
+
+    def forward_plane(at_layer):
+        for d in range(3):
+            in_plane(d, at_layer).wait_recv()
+            to_partner(d + 1, at_layer).start()
+
+    blocks_of(1)
+    forward_line(0)
     for copy in halos:
         copy.wait()
     item_ref[0:8] = halo_ref[0]
@@ -163,24 +206,59 @@
     block(blocks - 1, 0)
 
     share = rows // slabs
-    tail = jnp.concatenate([links_ref[rows : rows + 1], total_ref[0:1]], axis=0)
+    tail = jnp.concatenate(
+        [links_ref[rows : rows + 1], total_ref[0:1], jnp.zeros((6 - share, LANES), jnp.float32)], axis=0
+    )
     for d in range(slabs):
-        head_out[d, 0:share] = links_ref[d * share : (d + 1) * share]
-        head_out[d, share : share + 2] = tail
-        head_out[d, share + 2 : 8] = jnp.zeros((6 - share, LANES), jnp.float32)
-
-    exchange(slabs, me, head_out, head_in, head_send, head_recv, True)
-
-    def forward(k):
-        do_all(far(k), lambda c: c.wait_recv())
-        do_all(near(k), lambda c: c.start())
-
-    each(1, slabs // 2, forward)
-    exchange(slabs, me, head_out, head_in, head_send, head_recv, False)
-    head_ref[...] = jnp.sum(head_in[...], axis=0)
-    do_all(own_near, lambda c: c.wait())
-    each(1, slabs // 2, lambda k: do_all(near(k), lambda c: c.wait()))
-    each(1, slabs // 2, lambda k: do_all(far(k), lambda c: c.wait_send()))
+        at = (d % 2, d // PLANE, d // 2 % 4)
+        pair_out[at + (slice(0, share),)] = links_ref[d * share : (d + 1) * share]
+        pair_out[at + (slice(share, 8),)] = tail
+
+    pair = send(pair_out.at[1 - parity], pair_in, pair_sems.at[0], pair_sems.at[1], partner)
+    pair.start()
+    forward_line(1)
+    forward_plane(layer)
+    pair.wait()
+    line_out[...] = pair_out[parity] + pair_in[...]
+
+    def head_line(there, here):
+        return send(
+            line_out.at[there], line_in.at[layer], head_line_send.at[there], head_line_recv.at[here],
+            there * PLANE + low,
+        )
+
+    for o in others:
+        head_line(o, layer).start()
+    line_in[layer] = line_out[layer]
+    for k in range(2, depth - 1):
+        forward_line(k)
+    for o in others[:-1]:
+        forward_plane(o)
+    for o in others:
+        head_line(o, o).wait_recv()
+    plane_out[...] = jnp.sum(line_in[...], axis=0)
+
+    def head_plane(d):
+        to = me + steps[d]
+        return send(
+            plane_out.at[lax.rem(to // 2, 4)], plane_in.at[d], head_plane_send.at[d], head_plane_recv.at[d], to
+        )
+
+    for d in range(3):
+        head_plane(d).start()
+    for o in others[-1:]:
+        forward_plane(o)
+    for at_layer in [layer] + others:
+        for r in range(4):
+            to_partner(r, at_layer).wait()
+        for d in range(3):
+            in_plane(d, at_layer).wait_send()
+    for o in others:
+        along_line(o, layer).wait_send()
+        head_line(o, o).wait_send()
+    for d in range(3):
+        head_plane(d).wait()
+    head_ref[...] = plane_out[quad] + plane_in[0] + plane_in[1] + plane_in[2]
 
 
 def take_windows(code_ref, length, start):
@@ -203,7 +281,7 @@
     return value[0:32]
 
 
-def tile_kernel(rows, length, half, base_ref, all_items, all_sessions, count_ref, margin_ref, flat_ref, code_ref, key_ref):
+def tile_kernel(rows, length, half, base_ref, all_ref, count_ref, margin_ref, flat_ref, code_ref, key_ref):
     item_mask = (1 << ITEM_BITS) - 1
     base = base_ref[0]
     count_ref[...] = jnp.zeros_like(count_ref)
@@ -211,9 +289,11 @@
     band = 2 * half
     band_rows = band // LANES
     chunk = 8 * math.gcd(length // 8, 16)
-    slabs, blocks, unused_lanes = all_items.shape
+    slabs, blocks = all_ref.shape[0], all_ref.shape[1] * 2 // 3
     for n in range(slabs):
-        flat_ref[n * blocks : (n + 1) * blocks] = all_items[n] | (all_sessions[n].astype(jnp.int32) << ITEM_BITS)
+        paired = all_ref[n, blocks:]
+        sessions = jnp.concatenate([paired & 0xFFFF, paired >> 16], axis=0)
+        flat_ref[n * blocks : (n + 1) * blocks] = all_ref[n, 0:blocks] | (sessions << ITEM_BITS)
     per = length // LANES
     for r in range(per):
         code_ref[16 + r * LANES : 16 + (r + 1) * LANES] = flat_ref[pl.ds(r, LANES, stride=per), :].T
@@ -401,32 +481,41 @@
     length = total_events // LANES
 
     dma = pltpu.SemaphoreType.DMA
-    all_items, all_sessions, head = pl.pallas_call(
+    depth = slabs // PLANE
+    events, head = pl.pallas_call(
         functools.partial(gather_kernel, slabs, rows, blocks),
         out_shape=(
-            jax.ShapeDtypeStruct((slabs, blocks, LANES), jnp.int32),
-            jax.ShapeDtypeStruct((slabs, blocks, LANES), jnp.int16),
+            jax.ShapeDtypeStruct((slabs, blocks * 3 // 2, LANES), jnp.int32),
             jax.ShapeDtypeStruct((8, LANES), jnp.float32),
         ),
         in_specs=[VMEM],
-        out_specs=(VMEM, VMEM, VMEM),
+        out_specs=(VMEM, VMEM),
         scratch_shapes=[
-            pltpu.VMEM((blocks, LANES), jnp.int16),
+            pltpu.VMEM((blocks * 3 // 2, LANES), jnp.int32),
             pltpu.VMEM((4, 8, LANES), jnp.int32),
             pltpu.VMEM((blocks + 16, LANES), jnp.int32),
             pltpu.VMEM((blocks + 16, LANES), jnp.int32),
             pltpu.VMEM((rows + 8, LANES), jnp.float32),
             pltpu.VMEM((8, LANES), jnp.float32),
-            pltpu.VMEM((slabs, 8, LANES), jnp.float32),
-            pltpu.VMEM((slabs, 8, LANES), jnp.float32),
-            dma((slabs,)),
-            dma((slabs,)),
-            dma((slabs,)),
-            dma((slabs,)),
+            pltpu.VMEM((2, depth, 4, 8, LANES), jnp.float32),
+            pltpu.VMEM((depth, 4, 8, LANES), jnp.float32),
+            pltpu.VMEM((4, 8, LANES), jnp.float32),
+            pltpu.VMEM((3, 8, LANES), jnp.float32),
+            pltpu.VMEM((depth, 4, 8, LANES), jnp.float32),
+            pltpu.VMEM((depth, 4, 8, LANES), jnp.float32),
             dma((4,)),
             dma((4,)),
-            dma((slabs,)),
-            dma((slabs,)),
+            dma((depth,)),
+            dma((depth,)),
+            dma((3 * depth,)),
+            dma((3 * depth,)),
+            dma((4 * depth,)),
+            dma((4 * depth,)),
+            dma((2,)),
+            dma((3,)),
+            dma((3,)),
+            dma((depth,)),
+            dma((depth,)),
         ],
         compiler_params=pltpu.CompilerParams(
             collective_id=0, has_side_effects=True, vmem_limit_bytes=VMEM_GRANT
@@ -441,7 +530,7 @@
             jax.ShapeDtypeStruct((2, 2 * rows, half), jnp.float32),
             jax.ShapeDtypeStruct((2, band_rows, LANES), jnp.float32),
         ),
-        in_specs=[pl.BlockSpec(memory_space=pltpu.SMEM), VMEM, VMEM],
+        in_specs=[pl.BlockSpec(memory_space=pltpu.SMEM), VMEM],
         out_specs=(VMEM, VMEM),
         scratch_shapes=[
             pltpu.VMEM((length, LANES), jnp.int32),
@@ -450,7 +539,7 @@
         ],
         compiler_params=pltpu.CompilerParams(vmem_limit_bytes=VMEM_GRANT),
         name="tile_counts",
-    )(first_id.astype(jnp.int32)[None], all_items, all_sessions)
+    )(first_id.astype(jnp.int32)[None], events)
 
     own_rows = pl.pallas_call(
         functools.partial(sketch_kernel, slabs, rows, half, width, 1.0 / math.sqrt(total_events)),

time: 50.5 us -> 47.5 us (0.941)
  Pallas kernels: 49.1 us -> 46.3 us
    pallas_call x1, Pallas kernels: 15.8 us -> 14.2 us  [local(): pl.pallas_call(functools.partial(tile_kernel, rows, length, half), out_sh...]
    pallas_call x1, Pallas kernels: 20.9 us -> 19.8 us  [local(): pl.pallas_call(functools.partial(gather_kernel, slabs, rows, blocks), out...]
where the time goes in v1:
time: 47.5 us; the launch traced here: 47.6 us
  Pallas kernels  46.3 us (97%)
  other arithmetic  0.74 us (2%)
  local copies, waits for them, and re-layouts  0.6 us (1%)
    pallas_call x1, Pallas kernels, local(): pl.pallas_call(functools.partial(gather_kernel, slabs, rows, blocks), out...  19.8 us
    pallas_call x1, Pallas kernels, local(): pl.pallas_call(functools.partial(tile_kernel, rows, length, half), out_sh...  14.2 us
    pallas_call x1, Pallas kernels, local(): pl.pallas_call(functools.partial(sketch_kernel, slabs, rows, half, width,...  12.2 us

profile of v1, /device:TPU:0, one launch (start us, length us, event | category | flops | bytes accessed | tf_op | source)
XLA Modules:
  0.0 47.6 jit_solution(14999968701668987289)
XLA Ops:
  0.0 0.7 %pad_add_fusion.own_ref = s32[2,32,128]{2,1,0:T(8,128)S(1)} fusion(s32[1,32,128]{2,1,0:T(8,128)} %bitcast.3, s32[1,32,128]{2,1,0:T(8,128)} %bitcast.4), kind=kLoop, calls=%fused_computation | loop fusion | flops 8192 | bytes 65536 | tf_op jit(solution)/shard_map/stack | solution.py:524
  0.7 19.8 %gather_events.1 = (s32[32,48,128]{2,1,0:T(8,128)S(1)}, f32[8,128]{1,0:T(8,128)S(1)}) custom-call(s32[2,32,128]{2,1,0:T(8,128)S(1)} %pad_add_fusion.own_ref), custom_call_target="tpu_custom_call" | custom-call | tf_op jit(solution)/shard_map/gather_events/pallas_call | solution.py:485
  20.6 14.2 %tile_counts.1 = (f32[2,256,2048]{2,1,0:T(8,128)S(1)}, f32[2,32,128]{2,1,0:T(8,128)S(1)}) custom-call(s32[1]{0:T(128)} %bitcast.base_ref, s32[32,48,128]{2,1,0:T(8,128)S(1)} %get-tuple-element.9.all_ref), custom_call_target="tpu_custom_call" | custom-call | tf_op jit(solution)/shard_map/tile_counts/pallas_call | solution.py:527
  34.8 12.2 %sketch_tile.1 = f32[4,256]{1,0:T(4,128)S(1)} custom-call(f32[2,256,2048]{2,1,0:T(8,128)S(1)} %get-tuple-element.10.count_ref, f32[2,32,128]{2,1,0:T(8,128)S(1)} %get-tuple-element.11.margin_ref, f32[8,128]{1,0:T(8,128)S(1)} %get-tuple-element.12.head_ref, s32[15,262144]{1,0:T(8,128)} %bits_ref.1), custom_call_target="tpu_custom_call" | custom-call | tf_op jit(solution)/shard_map/sketch_tile/pallas_call | solution.py:544
  47.0 0.6 %copy.5 = f32[4,256]{1,0:T(4,128)} copy(f32[4,256]{1,0:T(4,128)S(1)} %sketch_tile.1) | data formatting | bytes 8192
